TPU v7x, 32 devices: a whole 2x2x4 slice. The times are simulated.
32 devices in a mesh: shots: 2 (over x), gz: 8 (over z, y), gy: 2 (over core).
Axes of the slice: x: 2, y: 2, z: 4, core: 2. Of those that a mesh axis runs over, the one named last changes fastest.
Arguments:
- pressure: float32 [256, 64, 512], P(('shots', 'gz'), 'gy'), parts along dimension 0, may hold values from -6 to 6
- previous: float32 [256, 64, 512], P(('shots', 'gz'), 'gy'), parts along dimension 0, may hold values from -6 to 6
- memory: float32 [3, 256, 64, 512], P(None, ('shots', 'gz'), 'gy'), parts along dimension 1, may hold values from -6 to 6
- courant: float32 [128, 64, 512], P('gz', 'gy'), may hold values from 0.05 to 0.25
- quality: float32 [128, 64, 512], P('gz', 'gy'), may hold values from 0.05 to 0.3
- sponge: int32 [128, 64, 512], P('gz', 'gy'), may hold values from 0 to 1, as said below
- relax_time: float32 [3], replicated, may hold values from 2 to 40
- receiver_cell: int32 [8, 2048], P(None, ('gz', 'gy')), may hold values from 0 to 262143
- receiver_weight: float32 [8, 2048], P(None, ('gz', 'gy')), may hold values from 0 to 1
- output_order: int32 [2048], P(('gz', 'gy')), may hold values from 0 to 2047, each once
Outputs:
- traces: float32 [48, 2048], P('shots', ('gz', 'gy')), parts along dimension 0
- pressure_out: float32 [256, 64, 512], P(('shots', 'gz'), 'gy'), parts along dimension 0
There are 2 independent parts, one for each index of `shots`. A program takes and returns all parts, laid end to end along the dimension named above; an argument that names none is the same for every part. Nothing has to cross between parts.
Inputs may be any that keep to these rules, and one draw needn't show every extreme that they name: sponge is 1 exactly in the first and last few inline cells, possibly the first and last few crossline cells and the deepest cells of the grid. `output_order`: each receiver appears once.
All inputs are finite; a program needn't handle non-finite values.
Results may differ from a plain program's by a relative error of at most 0.0001.
Values sent between devices are 32-bit elements; how exact they have to be, the bound alone decides.
A program may use at most 64 MiB of HBM per device.

v0:
```python
import jax
import jax.numpy as jnp
from jax import lax
from jax.sharding import PartitionSpec as P

STEPS = 8
WINDOWS = 3


sponge_rate = 0.2


def extended(block, sides, width):
    for axis, dim in sides:
        count = lax.axis_size(axis)
        forward = [(i, i + 1) for i in range(count - 1)]
        backward = [(target, source) for source, target in forward]
        low = lax.ppermute(
            lax.slice_in_dim(block, block.shape[dim] - width, None, axis=dim), axis, forward
        )
        high = lax.ppermute(lax.slice_in_dim(block, 0, width, axis=dim), axis, backward)
        block = jnp.concatenate([low, block, high], axis=dim)
    return block


def laplace(padded):
    middle = padded[1:-1, 1:-1, :]
    sides = jnp.pad(middle, ((0, 0), (0, 0), (1, 1)))
    summed = padded[2:, 1:-1, :] + padded[:-2, 1:-1, :]
    summed = summed + padded[1:-1, 2:, :] + padded[1:-1, :-2, :]
    summed = summed + sides[:, :, 2:] + sides[:, :, :-2]
    return summed - 6.0 * middle


def advance(padded, earlier, memory, courant, quality, damping, decays):
    stencil = laplace(padded)
    middle = padded[1:-1, 1:-1, :]
    retain = decays[:, None, None, None]
    memory = retain * memory + (1.0 - retain) * stencil[None]
    forcing = stencil + quality * (stencil - jnp.mean(memory, axis=0))
    updated = (2.0 * middle - (1.0 - damping) * earlier + courant * forcing) / (1.0 + damping)
    return (updated, memory)


def sample(field, receiver_cell, receiver_weight):
    picked = jnp.take(field.reshape(-1), receiver_cell, axis=0)
    return jnp.sum(picked * receiver_weight, axis=0)


def on_device(
    pressure,
    previous,
    memory,
    courant,
    quality,
    sponge,
    relax_time,
    receiver_cell,
    receiver_weight,
    output_order,
):
    damping = sponge_rate * sponge.astype(jnp.float32)
    decays = jnp.exp(-1.0 / relax_time)

    def one_step(carried, unused):
        current, earlier, mem_state = carried
        padded = extended(current, (("gz", 0), ("gy", 1)), 1)
        updated, mem_state = advance(padded, earlier, mem_state, courant, quality, damping, decays)
        return ((updated, current, mem_state), sample(updated, receiver_cell, receiver_weight))

    carried = (pressure, previous, memory)
    blocks = []
    for window in range(WINDOWS):
        carried, block = lax.scan(one_step, carried, None, length=STEPS)
        blocks.append(block)
    collected = lax.all_gather(jnp.concatenate(blocks, axis=0), ("gz", "gy"), axis=1, tiled=True)
    traces = jnp.take(collected, output_order, axis=1)
    return (traces, carried[0])


def solution(mesh):
    in_specs = (
        P(("shots", "gz"), "gy", None),
        P(("shots", "gz"), "gy", None),
        P(None, ("shots", "gz"), "gy", None),
        P("gz", "gy", None),
        P("gz", "gy", None),
        P("gz", "gy", None),
        P(),
        P(None, ("gz", "gy")),
        P(None, ("gz", "gy")),
        P(("gz", "gy")),
    )
    out_specs = (P("shots", ("gz", "gy")), P(("shots", "gz"), "gy", None))
    return jax.shard_map(
        on_device, mesh=mesh, in_specs=in_specs, out_specs=out_specs, check_vma=False
    )
```

profile of v0, /device:TPU:0, one launch (start us, length us, event | category | flops | bytes accessed | tf_op | source)
XLA Modules:
  0.0 742.4 jit_solution(16309842143547157312)
XLA Ops:
  0.6 4.1 copy.90
  8.8 241.3 %while.54 = (s32[]{:T(128)}, f32[16,32,512]{2,1,0:T(8,128)S(1)}, f32[16,32,512]{2,1,0:T(8,128)}, f32[3,16,32,512]{3,2,1,0:T(8,128)}, f32[8,128]{1,0:T(8,128)S(1)...) while((s32[]{:T(128)}, f32[16,32,512]{2,1,0:T(8,128)S(1)}, ...), condition=%wide.region_3.5_spmd, body=%wide.region_0.4_spmd.sunk | while | flops 8926085 | bytes 68446176 | solution.py:74
  8.8 4.9 collective-permute-start
  15.7 4.2 collective-permute-done.1
  33.7 6.2 gather_fusion
  40.0 4.3 collective-permute-start
  46.3 4.2 collective-permute-done.1
  64.3 6.2 gather_fusion
  70.6 3.4 collective-permute-start
  76.0 4.2 collective-permute-done.1
  94.1 6.2 gather_fusion
  100.3 4.3 collective-permute-start
  106.6 4.2 collective-permute-done.1
  124.7 6.2 gather_fusion
  130.9 3.4 collective-permute-start
  136.4 4.2 collective-permute-done.1
  154.4 6.2 gather_fusion
  160.6 4.3 collective-permute-start
  167.0 4.2 collective-permute-done.1
  185.0 6.2 gather_fusion
  191.3 3.4 collective-permute-start
  196.7 4.2 collective-permute-done.1
  214.7 6.2 gather_fusion
  225.8 4.2 collective-permute-done.1
  243.8 6.2 gather_fusion
  250.1 234.6 %while.55 = (s32[]{:T(128)}, f32[16,32,512]{2,1,0:T(8,128)S(1)}, f32[16,32,512]{2,1,0:T(8,128)}, f32[3,16,32,512]{3,2,1,0:T(8,128)}, f32[8,128]{1,0:T(8,128)S(1)...) while((s32[]{:T(128)}, f32[16,32,512]{2,1,0:T(8,128)S(1)}, ...), condition=%wide.region_7.9_spmd, body=%wide.region_4.8_spmd.sunk | while | flops 8926085 | bytes 68446176 | solution.py:74
  250.1 3.2 collective-permute-start.4
  255.3 4.2 collective-permute-done.5
  273.4 6.2 gather_fusion.1
  284.5 4.2 collective-permute-done.5
  302.5 6.2 gather_fusion.1
  308.7 3.2 collective-permute-start.4
  314.0 4.2 collective-permute-done.5
  332.0 6.2 gather_fusion.1
  343.1 4.2 collective-permute-done.5
  361.1 6.2 gather_fusion.1
  367.4 3.2 collective-permute-start.4
  372.6 4.2 collective-permute-done.5
  390.7 6.2 gather_fusion.1
  401.7 4.2 collective-permute-done.5
  419.8 6.2 gather_fusion.1
  426.0 3.2 collective-permute-start.4
  431.3 4.2 collective-permute-done.5
  449.3 6.2 gather_fusion.1
  460.4 4.2 collective-permute-done.5
  478.4 6.2 gather_fusion.1
  484.7 234.7 %while.56 = (s32[]{:T(128)}, f32[16,32,512]{2,1,0:T(8,128)S(1)}, f32[16,32,512]{2,1,0:T(8,128)}, f32[3,16,32,512]{3,2,1,0:T(8,128)}, f32[8,128]{1,0:T(8,128)S(1)...) while((s32[]{:T(128)}, f32[16,32,512]{2,1,0:T(8,128)S(1)}, ...), condition=%wide.region_11.13_spmd, body=%wide.region_8.12_spmd.sunk | while | flops 8926085 | bytes 68446176 | solution.py:74
  490.1 4.2 collective-permute-done.9
  508.1 6.2 gather_fusion.2
  519.2 4.2 collective-permute-done.9
  537.3 6.2 gather_fusion.2
  548.7 4.2 collective-permute-done.9
  566.8 6.2 gather_fusion.2
  577.9 4.2 collective-permute-done.9
  595.9 6.2 gather_fusion.2
  607.4 4.2 collective-permute-done.9
  625.4 6.2 gather_fusion.2
  636.5 4.2 collective-permute-done.9
  654.5 6.2 gather_fusion.2
  666.0 4.2 collective-permute-done.9
  684.1 6.2 gather_fusion.2
  695.1 4.2 collective-permute-done.9
  713.2 6.2 gather_fusion.2
  719.5 21.4 %all_gather.3 = f32[24,2048]{0,1:T(8,128)S(1)} all-gather(f32[24,128]{0,1:T(8,128)S(1)} %copy.20), channel_id=1, replica_groups=mesh['shots'=2,'gz'=8,'gy'=2] {'gz','gy'}, dimensions={1}, use_global_device_ids=true | all-gather | bytes 208896 | tf_op jit(solution)/shard_map/all_gather | solution.py:76
  (787 shorter events, 422.7 us)
Async XLA Ops:
  8.8 6.8 collective-permute-start
  13.7 6.2 collective-permute-start.1
  22.2 3.1 collective-permute-start.3
  40.0 6.2 collective-permute-start
  44.3 6.2 collective-permute-start.1
  52.9 3.1 collective-permute-start.3
  70.6 5.3 collective-permute-start
  74.0 6.2 collective-permute-start.1
  82.6 3.1 collective-permute-start.3
  100.3 6.2 collective-permute-start
  104.6 6.2 collective-permute-start.1
  113.2 3.1 collective-permute-start.3
  130.9 5.3 collective-permute-start
  134.4 6.2 collective-permute-start.1
  142.9 3.1 collective-permute-start.3
  160.6 6.2 collective-permute-start
  165.0 6.2 collective-permute-start.1
  173.5 3.1 collective-permute-start.3
  191.3 5.3 collective-permute-start
  194.7 6.2 collective-permute-start.1
  203.2 3.1 collective-permute-start.3
  221.0 4.7 collective-permute-start
  223.8 6.2 collective-permute-start.1
  232.4 3.1 collective-permute-start.3
  250.1 5.1 collective-permute-start.4
  253.3 6.2 collective-permute-start.5
  261.9 3.1 collective-permute-start.7
  279.6 4.7 collective-permute-start.4
  282.5 6.2 collective-permute-start.5
  291.0 3.1 collective-permute-start.7
  308.7 5.1 collective-permute-start.4
  312.0 6.2 collective-permute-start.5
  320.5 3.1 collective-permute-start.7
  338.3 4.7 collective-permute-start.4
  341.1 6.2 collective-permute-start.5
  349.6 3.1 collective-permute-start.7
  367.4 5.1 collective-permute-start.4
  370.6 6.2 collective-permute-start.5
  379.2 3.1 collective-permute-start.7
  396.9 4.7 collective-permute-start.4
  399.7 6.2 collective-permute-start.5
  408.3 3.1 collective-permute-start.7
  426.0 5.1 collective-permute-start.4
  429.3 6.2 collective-permute-start.5
  437.8 3.1 collective-permute-start.7
  455.5 4.7 collective-permute-start.4
  458.4 6.2 collective-permute-start.5
  466.9 3.1 collective-permute-start.7
  484.9 5.1 collective-permute-start.8
  488.1 6.2 collective-permute-start.9
  514.4 4.7 collective-permute-start.8
  517.2 6.2 collective-permute-start.9
  543.5 5.1 collective-permute-start.8
  546.8 6.2 collective-permute-start.9
  573.0 4.7 collective-permute-start.8
  575.9 6.2 collective-permute-start.9
  602.1 5.1 collective-permute-start.8
  605.4 6.2 collective-permute-start.9
  631.7 4.7 collective-permute-start.8
  634.5 6.2 collective-permute-start.9
  660.8 5.1 collective-permute-start.8
  664.0 6.2 collective-permute-start.9
  690.3 4.7 collective-permute-start.8
  693.1 6.2 collective-permute-start.9
  (160 other events, 650.1 us)
where the time goes:
time: 747 us; the launch traced here: 742 us
  local copies, waits for them, and re-layouts  219 us (29%)
  starting transfers between devices  173 us (23%)
  other arithmetic  168 us (22%)
  waiting for transfers between devices  156 us (21%)
  blocking collectives  21.4 us (3%)
    gather x24, local copies, waits for them, and re-layouts, sample(): picked = jnp.take(field.reshape(-1), receiver_cell, axis=0)  148 us
    ppermute x48, waiting for transfers between devices, extended(): lax.ppermute(lax.slice_in_dim(block, 0, width, axis=dim), axis, backward)  143 us
    ppermute x48, starting transfers between devices, extended(): lax.ppermute(lax.slice_in_dim(block, block.shape[dim] - width, None, axis...  111 us
    div x24, other arithmetic, advance(): (2.0 * middle - (1.0 - damping) * earlier + courant * forcing) / (1.0 + d...  70.4 us
    ppermute x48, starting transfers between devices, extended(): lax.ppermute(lax.slice_in_dim(block, 0, width, axis=dim), axis, backward)  62 us
    while x360, local copies, waits for them, and re-layouts  59.4 us
    sub x24, other arithmetic, laplace(): return summed - 6.0 * middle  57.6 us
    reduce_sum x24, other arithmetic, advance(): forcing = stencil + quality * (stencil - jnp.mean(memory, axis=0))  38.6 us
  transfers between devices with their start and end apart: 96, of which 72 were waited for; matrix products, arithmetic and copies ran while one was open for 0% of the time, Pallas kernels for 0%

commit v1 on v0

v1 whole, which is shorter than its diff:
```python
import jax
import jax.numpy as jnp
from jax import lax
from jax.experimental import pallas as pl
from jax.experimental.pallas import tpu as pltpu
from jax.sharding import PartitionSpec as P

TIME = 24
MECH = 3
SPONGE_RATE = 0.2
SUB = 8
LANE = 128
MESH = pl.DeviceIdType.MESH


def to_rows(block):
    y, x = block.shape[-2:]
    lead = block.size // (y * x)
    tiles = block.reshape(lead, y // SUB, SUB, x // LANE, LANE)
    return tiles.transpose(0, 1, 3, 2, 4).reshape(block.size // LANE, LANE)


def from_rows(rows, shape):
    z, y, x = shape
    tiles = rows.reshape(z, y // SUB, x // LANE, SUB, LANE)
    return tiles.transpose(0, 1, 3, 2, 4).reshape(shape)


def make_kernel(cz, cy, nx, n_gz, n_gy, corners, recs):
    yt, xt = cy // SUB, nx // LANE
    plane = cy * nx // LANE
    block = cz * plane
    slot = (cz + 2) * plane + SUB
    slots = TIME + 2

    def kernel(
        pressure, previous, memory, courant, quality, sponge, decays, rows, lanes, weights,
        samples, pressure_out,
        hist, mem, ca, cb, sp, inv2, ysend, yrecv,
        load_sem, zsend_sem, zrecv_sem, ysend_sem, yrecv_sem, out_sem,
    ):
        gz = lax.axis_index("gz")
        gy = lax.axis_index("gy")
        z_has = (gz > 0, gz < n_gz - 1)
        y_has = (gy > 0, gy < n_gy - 1)
        z_dev = (jnp.maximum(gz - 1, 0), jnp.minimum(gz + 1, n_gz - 1))
        y_dev = (jnp.maximum(gy - 1, 0), jnp.minimum(gy + 1, n_gy - 1))

        def hist_at(level, p):
            return pl.multiple_of(level * slot + p * plane, SUB)

        loads = [
            pltpu.make_async_copy(pressure, hist.at[pl.ds(slot + plane, block)], load_sem.at[0]),
            pltpu.make_async_copy(courant, ca, load_sem.at[1]),
            pltpu.make_async_copy(quality, cb, load_sem.at[2]),
            pltpu.make_async_copy(sponge, sp, load_sem.at[3]),
            pltpu.make_async_copy(previous, hist.at[pl.ds(plane, block)], load_sem.at[4]),
            pltpu.make_async_copy(memory, mem, load_sem.at[5]),
        ]
        for copy in loads:
            copy.start()

        barrier = pltpu.get_barrier_semaphore()
        for side in range(2):
            @pl.when(z_has[side])
            def _():
                pl.semaphore_signal(barrier, inc=1, device_id={"gz": z_dev[side]}, device_id_type=MESH)

            @pl.when(y_has[side])
            def _():
                pl.semaphore_signal(barrier, inc=1, device_id={"gy": y_dev[side]}, device_id_type=MESH)

        zero = jnp.zeros((SUB, LANE), jnp.float32)
        for side in range(2):
            @pl.when(jnp.logical_not(z_has[side]))
            def _():
                def fill(level, carry):
                    base = hist_at(level, side * (cz + 1))
                    for i in range(plane // SUB):
                        hist[pl.ds(base + i * SUB, SUB), :] = zero
                    return carry
                lax.fori_loop(1, slots, fill, 0)

            @pl.when(jnp.logical_not(y_has[side]))
            def _():
                def fill(level, carry):
                    for q in range(cz):
                        yrecv[level, side, q] = jnp.zeros((xt, LANE), jnp.float32)
                    return carry
                lax.fori_loop(1, slots, fill, 0)

        peers = sum(has.astype(jnp.int32) for has in z_has + y_has)
        pl.semaphore_wait(barrier, peers)

        part = xt * SUB

        def z_copy(level, side, chunk):
            source = hist_at(level, (1, cz)[side]) + chunk * part
            target = hist_at(level, (cz + 1, 0)[side]) + chunk * part
            par = level % 2
            return pltpu.make_async_remote_copy(
                src_ref=hist.at[pl.ds(pl.multiple_of(source, SUB), part)],
                dst_ref=hist.at[pl.ds(pl.multiple_of(target, SUB), part)],
                send_sem=zsend_sem.at[par, side, chunk],
                recv_sem=zrecv_sem.at[par, side, chunk],
                device_id={"gz": z_dev[side]},
                device_id_type=MESH,
            )

        def y_copy(level, side, piece):
            start, count = ((0, 2), (2, cz - 2))[piece]
            par = level % 2
            return pltpu.make_async_remote_copy(
                src_ref=ysend.at[level, side, pl.ds(start, count)],
                dst_ref=yrecv.at[level, 1 - side, pl.ds(start, count)],
                send_sem=ysend_sem.at[par, side, piece],
                recv_sem=yrecv_sem.at[par, side, piece],
                device_id={"gy": y_dev[side]},
                device_id_type=MESH,
            )

        def send(copy_of, has, level, index, go=None):
            for side in range(2):
                @pl.when(has[side] if go is None else has[side] & go)
                def _():
                    copy_of(level, side, index).start()

        def settle(copy_of, has, level, index):
            for side in range(2):
                @pl.when(has[side])
                def _():
                    copy_of(level, side, index).wait_send()
                    copy_of(level, 1 - side, index).wait_recv()

        def keep_rows(level, q, b, x, tile):
            if b == 0:
                ysend[level, 0, q, x:x + 1, :] = tile[0:1, :]
            if b == yt - 1:
                ysend[level, 1, q, x:x + 1, :] = tile[SUB - 1:SUB, :]

        loads[0].wait()
        for chunk in range(yt):
            send(z_copy, z_has, 1, chunk)

        def first_rows(z, q):
            base = hist_at(1, z + 1)
            for b in sorted({0, yt - 1}):
                for x in range(xt):
                    keep_rows(1, q, b, x, hist[pl.ds(base + (b * xt + x) * SUB, SUB), :])

        first_rows(0, 0)
        first_rows(cz - 1, 1)
        send(y_copy, y_has, 1, 0)

        def first_loop(z, carry):
            first_rows(z, z + 1)
            return carry
        lax.fori_loop(1, cz - 1, first_loop, 0)
        send(y_copy, y_has, 1, 1)

        for copy in loads[1:4]:
            copy.wait()

        def coefficients(i, carry):
            for j in range(4):
                at = pl.ds(pl.multiple_of((i * 4 + j) * SUB, SUB), SUB)
                two = 2.0 / (1.0 + SPONGE_RATE * sp[at, :].astype(jnp.float32))
                scaled = ca[at, :] * (0.5 * two)
                attenuation = cb[at, :]
                inv2[at, :] = two
                ca[at, :] = scaled * (1.0 + attenuation)
                cb[at, :] = scaled * attenuation * (1.0 / MECH)
            return carry
        lax.fori_loop(0, block // (4 * SUB), coefficients, 0)
        for copy in loads[4:]:
            copy.wait()

        lane = lax.broadcasted_iota(jnp.int32, (SUB, LANE), 1)
        sub = lax.broadcasted_iota(jnp.int32, (SUB, LANE), 0)
        lane_first, lane_last = lane == 0, lane == LANE - 1
        sub_first, sub_last = sub == 0, sub == SUB - 1
        retain = [decays[m] for m in range(MECH)]
        renew = [1.0 - r for r in retain]

        def advance(t, z, q, bands):
            now = hist_at(t + 1, z + 1)
            before = hist_at(t, z + 1)
            after = hist_at(t + 2, z + 1)
            cell = pl.multiple_of(z * plane, SUB)

            def tile_of(ref, base, b, x):
                return ref[pl.ds(pl.multiple_of(base + (b * xt + x) * SUB, SUB), SUB), :]

            for b in bands:
                mids = [tile_of(hist, now, b, x) for x in range(xt)]
                right = [pltpu.roll(v, 1, 1) for v in mids]
                left = [pltpu.roll(v, LANE - 1, 1) for v in mids]
                for x in range(xt):
                    c = mids[x]
                    xm = jnp.where(lane_first, right[x - 1] if x > 0 else 0.0, right[x])
                    xp = jnp.where(lane_last, left[x + 1] if x < xt - 1 else 0.0, left[x])
                    if b > 0:
                        edge = pltpu.roll(tile_of(hist, now, b - 1, x), 1, 0)
                    else:
                        edge = jnp.broadcast_to(yrecv[t + 1, 0, q, x:x + 1, :], (SUB, LANE))
                    ym = jnp.where(sub_first, edge, pltpu.roll(c, 1, 0))
                    if b < yt - 1:
                        edge = pltpu.roll(tile_of(hist, now, b + 1, x), SUB - 1, 0)
                    else:
                        edge = jnp.broadcast_to(yrecv[t + 1, 1, q, x:x + 1, :], (SUB, LANE))
                    yp = jnp.where(sub_last, edge, pltpu.roll(c, SUB - 1, 0))
                    zm = tile_of(hist, now - plane, b, x)
                    zp = tile_of(hist, now + plane, b, x)
                    s = ((zp + zm) + (yp + ym)) + (xp + xm) - 6.0 * c
                    total = None
                    for m in range(MECH):
                        at = pl.ds(pl.multiple_of(m * block + cell + (b * xt + x) * SUB, SUB), SUB)
                        value = retain[m] * mem[at, :] + renew[m] * s
                        mem[at, :] = value
                        total = value if total is None else total + value
                    e = tile_of(hist, before, b, x)
                    u = (e + tile_of(inv2, cell, b, x) * (c - e)) + (
                        tile_of(ca, cell, b, x) * s - tile_of(cb, cell, b, x) * total
                    )
                    hist[pl.ds(pl.multiple_of(after + (b * xt + x) * SUB, SUB), SUB), :] = u
                    keep_rows(t + 2, q, b, x, u)

        def step(t, carry):
            go = t < TIME - 1
            settle(y_copy, y_has, t + 1, 0)
            for b in range(yt):
                settle(z_copy, z_has, t + 1, b)
                advance(t, 0, 0, [b])
                advance(t, cz - 1, 1, [b])
                send(z_copy, z_has, t + 2, b, go)
            send(y_copy, y_has, t + 2, 0, go)
            settle(y_copy, y_has, t + 1, 1)

            def inner(z, c):
                advance(t, z, z + 1, list(range(yt)))
                return c
            lax.fori_loop(1, cz - 1, inner, 0)
            send(y_copy, y_has, t + 2, 1, go)
            return carry
        lax.fori_loop(0, TIME, step, 0)

        result = pltpu.make_async_copy(
            hist.at[pl.ds((TIME + 1) * slot + plane, block)], pressure_out, out_sem)
        result.start()

        groups = TIME // SUB

        def record(r, found):
            sums = [jnp.zeros((SUB, LANE), jnp.float32) for _ in range(groups)]
            for c in range(corners):
                row = rows[c * recs + r]
                mask = jnp.where(lane == lanes[c * recs + r], weights[c * recs + r], 0.0)
                for g in range(groups):
                    start = (2 + g * SUB) * slot + plane + row
                    sums[g] = sums[g] + mask * hist[pl.ds(start, SUB, stride=slot), :]
            return tuple(
                jnp.where(lane == r, jnp.sum(sums[g], axis=1, keepdims=True), found[g])
                for g in range(groups))
        found = lax.fori_loop(
            0, recs, record,
            tuple(jnp.zeros((SUB, LANE), jnp.float32) for _ in range(groups)), unroll=4)
        for g in range(groups):
            samples[pl.ds(g * SUB, SUB), :] = found[g]
        result.wait()

    f32 = jnp.float32
    any_spec = pl.BlockSpec(memory_space=pl.ANY)
    smem = pl.BlockSpec(memory_space=pltpu.SMEM)
    return pl.pallas_call(
        kernel,
        out_shape=(
            jax.ShapeDtypeStruct((TIME, recs), f32),
            jax.ShapeDtypeStruct((block, LANE), f32),
        ),
        in_specs=[any_spec] * 6 + [smem] * 4,
        out_specs=(pl.BlockSpec(memory_space=pltpu.VMEM), any_spec),
        scratch_shapes=[
            pltpu.VMEM((slots * slot, LANE), f32),
            pltpu.VMEM((MECH * block, LANE), f32),
            pltpu.VMEM((block, LANE), f32),
            pltpu.VMEM((block, LANE), f32),
            pltpu.VMEM((block, LANE), jnp.int32),
            pltpu.VMEM((block, LANE), f32),
            pltpu.VMEM((slots, 2, cz, xt, LANE), f32),
            pltpu.VMEM((slots, 2, cz, xt, LANE), f32),
            pltpu.SemaphoreType.DMA((6,)),
            pltpu.SemaphoreType.DMA((2, 2, yt)),
            pltpu.SemaphoreType.DMA((2, 2, yt)),
            pltpu.SemaphoreType.DMA((2, 2, 2)),
            pltpu.SemaphoreType.DMA((2, 2, 2)),
            pltpu.SemaphoreType.DMA,
        ],
        compiler_params=pltpu.CompilerParams(
            collective_id=0, has_side_effects=True, vmem_limit_bytes=60 * 1024 * 1024,
        ),
    )


def solution(mesh):
    n_gz, n_gy = mesh.shape["gz"], mesh.shape["gy"]

    def on_device(
        pressure, previous, memory, courant, quality, sponge, relax_time,
        receiver_cell, receiver_weight, output_order,
    ):
        cz, cy, nx = pressure.shape
        corners, recs = receiver_cell.shape
        decays = jnp.exp(-1.0 / relax_time)
        x = receiver_cell % nx
        y = (receiver_cell // nx) % cy
        z = receiver_cell // (nx * cy)
        rows = ((z * (cy // SUB) + y // SUB) * (nx // LANE) + x // LANE) * SUB + y % SUB
        run = make_kernel(cz, cy, nx, n_gz, n_gy, corners, recs)
        samples, out = run(
            to_rows(pressure), to_rows(previous), to_rows(memory), to_rows(courant),
            to_rows(quality), to_rows(sponge), decays,
            rows.reshape(-1), (x % LANE).reshape(-1), receiver_weight.reshape(-1),
        )
        collected = lax.all_gather(samples, ("gz", "gy"), axis=1, tiled=True)
        pick = lax.broadcasted_iota(jnp.int32, (collected.shape[1], recs), 0) == output_order[None, :]
        traces = jnp.dot(collected, pick.astype(jnp.float32), precision=lax.Precision.HIGHEST)
        return traces, from_rows(out, (cz, cy, nx))

    in_specs = (
        P(("shots", "gz"), "gy", None),
        P(("shots", "gz"), "gy", None),
        P(None, ("shots", "gz"), "gy", None),
        P("gz", "gy", None),
        P("gz", "gy", None),
        P("gz", "gy", None),
        P(),
        P(None, ("gz", "gy")),
        P(None, ("gz", "gy")),
        P(("gz", "gy")),
    )
    out_specs = (P("shots", ("gz", "gy")), P(("shots", "gz"), "gy", None))
    return jax.shard_map(
        on_device, mesh=mesh, in_specs=in_specs, out_specs=out_specs, check_vma=False
    )
```

time: 747 us -> 123 us (0.16)
  local copies, waits for them, and re-layouts: 219 us -> 2.29 us
  starting transfers between devices: 173 us -> 0 us
  other arithmetic: 168 us -> 2.46 us
  waiting for transfers between devices: 156 us -> 0 us
  Pallas kernels: 0 us -> 95.8 us
    ppermute x96 -> x0, starting transfers between devices: 173 us -> none  [the longest x48 111 us: extended(): lax.ppermute(lax.slice_in_dim(block, block.shape[dim] - width, None, axis...]
    ppermute x96 -> x0, waiting for transfers between devices: 156 us -> none  [the longest x48 143 us: extended(): lax.ppermute(lax.slice_in_dim(block, 0, width, axis=dim), axis, backward)]
    gather x25 -> x0, local copies, waits for them, and re-layouts: 148 us -> none  [the longest x24 148 us: sample(): picked = jnp.take(field.reshape(-1), receiver_cell, axis=0)]
    pallas_call x0 -> x1, Pallas kernels: none -> 95.8 us  [on_device(): run(to_rows(pressure), to_rows(previous), to_rows(memory), to_rows(couran...]
    div x24 -> x0, other arithmetic: 70.4 us -> none  [advance(): (2.0 * middle - (1.0 - damping) * earlier + courant * forcing) / (1.0 + d...]
    while x360 -> x0, local copies, waits for them, and re-layouts: 59.4 us -> none
    sub x48 -> x0, other arithmetic: 57.7 us -> none  [the longest x24 57.6 us: laplace(): return summed - 6.0 * middle]
    reduce_sum x48 -> x0, other arithmetic: 39.2 us -> none  [the longest x24 38.6 us: advance(): forcing = stencil + quality * (stencil - jnp.mean(memory, axis=0))]
  transfers between devices with their start and end apart: 96 -> 0, of which waited for: 72 -> 0; matrix products, arithmetic and copies ran while one was open for 0% -> 0% of each run, Pallas kernels for 0% -> 0%
where the time goes in v1:
time: 123 us
  Pallas kernels  95.8 us (78%)
  blocking collectives  20.5 us (17%)
  other arithmetic  2.46 us (2%)
  local copies, waits for them, and re-layouts  2.29 us (2%)
    pallas_call x1, Pallas kernels, on_device(): run(to_rows(pressure), to_rows(previous), to_rows(memory), to_rows(couran...  95.8 us
    all_gather x1, blocking collectives, on_device(): collected = lax.all_gather(samples, ('gz', 'gy'), axis=1, tiled=True)  20.5 us

profile of v1, /device:TPU:0, one launch (start us, length us, event | category | flops | bytes accessed | tf_op | source)
XLA Modules:
  0.0 122.8 jit_solution(18098567676973640221)
XLA Ops:
  0.6 1.2 divide_exponential_fusion.decays
  1.8 1.3 %fusion.11 = (s32[1024]{0:T(1024)}, s32[1024]{0:T(1024)}) fusion(s32[8,128]{1,0:T(8,128)} %param.17), kind=kLoop, calls=%fused_computation.33 | loop fusion | flops 86016 | bytes 12288 | tf_op jit(solution)/shard_map/reshape | solution.py:322
  3.1 0.0 copy-start
  3.1 95.8 %shard_map.113 = (f32[24,128]{1,0:T(8,128)}, f32[2048,128]{1,0:T(8,128)}) custom-call(f32[2048,128]{1,0:T(8,128)} %bitcast.42, f32[2048,128]{1,0:T(8,128)} %bitcast.43, f32[6144,128]{1,0:T(8,128)} %bitcast.41, f32[2048,128]{1,0:T(8,128)} %bitcast.44, f32[2048,128]{1,0:T(8,128)} %bitcast.45, s32[2048,128]{1,0:T(8,128)} %bitcast.46, ...), custom_call_target="tpu_custom_call" | custom-call | tf_op jit(solution)/shard_map/pallas_call | solution.py:319
  98.9 20.5 %all_gather.3 = f32[24,2048]{1,0:T(8,128)S(1)} all-gather(f32[24,128]{1,0:T(8,128)} %get-tuple-element.4), channel_id=1, replica_groups=mesh['shots'=2,'gz'=8,'gy'=2] {'gz','gy'}, dimensions={1}, use_global_device_ids=true | all-gather | bytes 208896 | tf_op jit(solution)/shard_map/all_gather | solution.py:324
  119.4 0.0 copy-done
  119.4 1.1 fusion
  120.5 2.3 %copy.13 = f32[16,32,512]{2,1,0:T(8,128)} copy(f32[16,32,512]{2,1,0:T(8,128)} %bitcast.47) | data formatting | bytes 2097152
Async XLA Ops:
  3.1 116.3 %copy-start = (s32[128]{0:T(128)S(1)}, s32[128]{0:T(128)}, u32[]{:S(2)}) copy-start(s32[128]{0:T(128)} %param.19) | copy-start | bytes 1540

commit v2 on v1

--- a/solution.py
+++ b/solution.py
@@ -30,14 +30,15 @@
     yt, xt = cy // SUB, nx // LANE
     plane = cy * nx // LANE
     block = cz * plane
-    slot = (cz + 2) * plane + SUB
+    slot = block + SUB
+    n_dev = n_gz * n_gy
     slots = TIME + 2
 
     def kernel(
-        pressure, previous, memory, courant, quality, sponge, decays, rows, lanes, weights,
-        samples, pressure_out,
-        hist, mem, ca, cb, sp, inv2, ysend, yrecv,
-        load_sem, zsend_sem, zrecv_sem, ysend_sem, yrecv_sem, out_sem,
+        pressure, previous, memory, courant, quality, sponge, relax, rows, lanes, weights, order,
+        traces, pressure_out,
+        hist, zrecv, mem, ca, cb, sp, inv2, ysend, yrecv, samples, gathered, onehot,
+        load_sem, zsend_sem, zrecv_sem, ysend_sem, yrecv_sem, gsend_sem, grecv_sem, out_sem,
     ):
         gz = lax.axis_index("gz")
         gy = lax.axis_index("gy")
@@ -46,38 +47,43 @@
         z_dev = (jnp.maximum(gz - 1, 0), jnp.minimum(gz + 1, n_gz - 1))
         y_dev = (jnp.maximum(gy - 1, 0), jnp.minimum(gy + 1, n_gy - 1))
 
+        me = gz * n_gy + gy
+
+        def device(index):
+            return {"gz": index // n_gy, "gy": index % n_gy}
+
         def hist_at(level, p):
             return pl.multiple_of(level * slot + p * plane, SUB)
 
+        def halo_at(level, side):
+            return pl.multiple_of((level * 2 + side) * plane, SUB)
+
         loads = [
-            pltpu.make_async_copy(pressure, hist.at[pl.ds(slot + plane, block)], load_sem.at[0]),
+            pltpu.make_async_copy(pressure, hist.at[pl.ds(slot, block)], load_sem.at[0]),
             pltpu.make_async_copy(courant, ca, load_sem.at[1]),
             pltpu.make_async_copy(quality, cb, load_sem.at[2]),
             pltpu.make_async_copy(sponge, sp, load_sem.at[3]),
-            pltpu.make_async_copy(previous, hist.at[pl.ds(plane, block)], load_sem.at[4]),
+            pltpu.make_async_copy(previous, hist.at[pl.ds(0, block)], load_sem.at[4]),
             pltpu.make_async_copy(memory, mem, load_sem.at[5]),
         ]
         for copy in loads:
             copy.start()
 
         barrier = pltpu.get_barrier_semaphore()
-        for side in range(2):
-            @pl.when(z_has[side])
-            def _():
-                pl.semaphore_signal(barrier, inc=1, device_id={"gz": z_dev[side]}, device_id_type=MESH)
-
-            @pl.when(y_has[side])
-            def _():
-                pl.semaphore_signal(barrier, inc=1, device_id={"gy": y_dev[side]}, device_id_type=MESH)
+        def greet(k, carry):
+            pl.semaphore_signal(
+                barrier, inc=1, device_id=device((me + k) % n_dev), device_id_type=MESH)
+            return carry
+        lax.fori_loop(1, n_dev, greet, 0)
 
         zero = jnp.zeros((SUB, LANE), jnp.float32)
         for side in range(2):
             @pl.when(jnp.logical_not(z_has[side]))
             def _():
                 def fill(level, carry):
-                    base = hist_at(level, side * (cz + 1))
+                    base = halo_at(level, side)
                     for i in range(plane // SUB):
-                        hist[pl.ds(base + i * SUB, SUB), :] = zero
+                        zrecv[pl.ds(base + i * SUB, SUB), :] = zero
                     return carry
                 lax.fori_loop(1, slots, fill, 0)
 
@@ -89,18 +95,17 @@
                     return carry
                 lax.fori_loop(1, slots, fill, 0)
 
-        peers = sum(has.astype(jnp.int32) for has in z_has + y_has)
-        pl.semaphore_wait(barrier, peers)
+        pl.semaphore_wait(barrier, n_dev - 1)
 
         part = xt * SUB
 
         def z_copy(level, side, chunk):
-            source = hist_at(level, (1, cz)[side]) + chunk * part
-            target = hist_at(level, (cz + 1, 0)[side]) + chunk * part
+            source = hist_at(level, (0, cz - 1)[side]) + chunk * part
+            target = halo_at(level, 1 - side) + chunk * part
             par = level % 2
             return pltpu.make_async_remote_copy(
                 src_ref=hist.at[pl.ds(pl.multiple_of(source, SUB), part)],
-                dst_ref=hist.at[pl.ds(pl.multiple_of(target, SUB), part)],
+                dst_ref=zrecv.at[pl.ds(pl.multiple_of(target, SUB), part)],
                 send_sem=zsend_sem.at[par, side, chunk],
                 recv_sem=zrecv_sem.at[par, side, chunk],
                 device_id={"gz": z_dev[side]},
@@ -143,7 +148,7 @@
             send(z_copy, z_has, 1, chunk)
 
         def first_rows(z, q):
-            base = hist_at(1, z + 1)
+            base = hist_at(1, z)
             for b in sorted({0, yt - 1}):
                 for x in range(xt):
                     keep_rows(1, q, b, x, hist[pl.ds(base + (b * xt + x) * SUB, SUB), :])
@@ -179,14 +184,18 @@
         sub = lax.broadcasted_iota(jnp.int32, (SUB, LANE), 0)
         lane_first, lane_last = lane == 0, lane == LANE - 1
         sub_first, sub_last = sub == 0, sub == SUB - 1
-        retain = [decays[m] for m in range(MECH)]
+        retain = [jnp.exp(-1.0 / jnp.full((SUB, LANE), relax[m], jnp.float32)) for m in range(MECH)]
         renew = [1.0 - r for r in retain]
 
         def advance(t, z, q, bands):
-            now = hist_at(t + 1, z + 1)
-            before = hist_at(t, z + 1)
-            after = hist_at(t + 2, z + 1)
+            now = hist_at(t + 1, z)
+            before = hist_at(t, z)
+            after = hist_at(t + 2, z)
             cell = pl.multiple_of(z * plane, SUB)
+            first = isinstance(z, int) and z == 0
+            last = isinstance(z, int) and z == cz - 1
+            below = (zrecv, halo_at(t + 1, 0)) if first else (hist, now - plane)
+            above = (zrecv, halo_at(t + 1, 1)) if last else (hist, now + plane)
 
             def tile_of(ref, base, b, x):
                 return ref[pl.ds(pl.multiple_of(base + (b * xt + x) * SUB, SUB), SUB), :]
@@ -209,8 +218,8 @@
                     else:
                         edge = jnp.broadcast_to(yrecv[t + 1, 1, q, x:x + 1, :], (SUB, LANE))
                     yp = jnp.where(sub_last, edge, pltpu.roll(c, SUB - 1, 0))
-                    zm = tile_of(hist, now - plane, b, x)
-                    zp = tile_of(hist, now + plane, b, x)
+                    zm = tile_of(*below, b, x)
+                    zp = tile_of(*above, b, x)
                     s = ((zp + zm) + (yp + ym)) + (xp + xm) - 6.0 * c
                     total = None
                     for m in range(MECH):
@@ -241,31 +250,83 @@
                 return c
             lax.fori_loop(1, cz - 1, inner, 0)
             send(y_copy, y_has, t + 2, 1, go)
-            return carry
+
+            @pl.when(t >= SUB)
+            def _():
+                found_at(t // SUB - 1, (t % SUB) * share, share, 4)
+            return carry
+
+        groups = TIME // SUB
+        share = recs // SUB
+
+        def found_at(g, begin, count, unroll):
+            at = pl.ds(pl.multiple_of(g * SUB, SUB), SUB)
+            level = (2 + g * SUB) * slot
+
+            def record(i, found):
+                r = begin + i
+                sums = jnp.zeros((SUB, LANE), jnp.float32)
+                for c in range(corners):
+                    mask = jnp.where(lane == lanes[c * recs + r], weights[c * recs + r], 0.0)
+                    row = level + rows[c * recs + r]
+                    sums = sums + mask * hist[pl.ds(row, SUB, stride=slot), :]
+                return jnp.where(lane == r, jnp.sum(sums, axis=1, keepdims=True), found)
+            samples[at, :] = lax.fori_loop(0, count, record, samples[at, :], unroll=unroll)
+
+        samples[...] = jnp.zeros((TIME, recs), jnp.float32)
         lax.fori_loop(0, TIME, step, 0)
 
         result = pltpu.make_async_copy(
-            hist.at[pl.ds((TIME + 1) * slot + plane, block)], pressure_out, out_sem)
+            hist.at[pl.ds((TIME + 1) * slot, block)], pressure_out, out_sem)
         result.start()
-
-        groups = TIME // SUB
-
-        def record(r, found):
-            sums = [jnp.zeros((SUB, LANE), jnp.float32) for _ in range(groups)]
-            for c in range(corners):
-                row = rows[c * recs + r]
-                mask = jnp.where(lane == lanes[c * recs + r], weights[c * recs + r], 0.0)
-                for g in range(groups):
-                    start = (2 + g * SUB) * slot + plane + row
-                    sums[g] = sums[g] + mask * hist[pl.ds(start, SUB, stride=slot), :]
-            return tuple(
-                jnp.where(lane == r, jnp.sum(sums[g], axis=1, keepdims=True), found[g])
-                for g in range(groups))
-        found = lax.fori_loop(
-            0, recs, record,
-            tuple(jnp.zeros((SUB, LANE), jnp.float32) for _ in range(groups)), unroll=4)
-        for g in range(groups):
-            samples[pl.ds(g * SUB, SUB), :] = found[g]
+        found_at(groups - 1, 0, recs, 8)
+
+        def g_copy(k, owner):
+            return pltpu.make_async_remote_copy(
+                src_ref=samples,
+                dst_ref=gathered.at[pl.ds(pl.multiple_of(owner * TIME, SUB), TIME)],
+                send_sem=gsend_sem.at[k],
+                recv_sem=grecv_sem.at[k],
+                device_id=device((me + k) % n_dev),
+                device_id_type=MESH,
+            )
+
+        def push(k, carry):
+            g_copy(k, me).start()
+            return carry
+        lax.fori_loop(1, n_dev, push, 0)
+        gathered[pl.ds(pl.multiple_of(me * TIME, SUB), TIME), :] = samples[...]
+
+        wanted = jnp.broadcast_to(order[0:1, :], (recs, recs))
+        receiver = lax.broadcasted_iota(jnp.int32, (recs, recs), 0)
+
+        def mark(d, carry):
+            hit = receiver + d * recs == wanted
+            onehot[pl.ds(pl.multiple_of(d * recs, recs), recs), :] = jnp.where(
+                hit, 1.0, 0.0).astype(jnp.bfloat16)
+            return carry
+        lax.fori_loop(0, n_dev, mark, 0)
+
+        def arrive(k, carry):
+            g_copy(k, me).wait_send()
+            g_copy(k, (me + n_dev - k) % n_dev).wait_recv()
+            return carry
+        lax.fori_loop(1, n_dev, arrive, 0)
+
+        def reorder(d, total):
+            value = gathered[pl.ds(pl.multiple_of(d * TIME, SUB), TIME), :]
+            high = value.astype(jnp.bfloat16).astype(jnp.float32)
+            rest = value - high
+            mid = rest.astype(jnp.bfloat16).astype(jnp.float32)
+            spare = jnp.zeros((-3 * TIME % 16, recs), jnp.float32)
+            parts = [high, mid, rest - mid] + ([spare] if spare.shape[0] else [])
+            stacked = jnp.concatenate(parts, axis=0).astype(jnp.bfloat16)
+            pick = onehot[pl.ds(pl.multiple_of(d * recs, recs), recs), :]
+            return total + jnp.dot(stacked, pick, preferred_element_type=jnp.float32)
+        height = 3 * TIME + (-3 * TIME % 16)
+        total = lax.fori_loop(
+            0, n_dev, reorder, jnp.zeros((height, recs), jnp.float32), unroll=4)
+        traces[...] = (total[0:TIME] + total[TIME:2 * TIME]) + total[2 * TIME:3 * TIME]
         result.wait()
 
     f32 = jnp.float32
@@ -277,10 +338,11 @@
             jax.ShapeDtypeStruct((TIME, recs), f32),
             jax.ShapeDtypeStruct((block, LANE), f32),
         ),
-        in_specs=[any_spec] * 6 + [smem] * 4,
+        in_specs=[any_spec] * 6 + [smem] * 4 + [pl.BlockSpec(memory_space=pltpu.VMEM)],
         out_specs=(pl.BlockSpec(memory_space=pltpu.VMEM), any_spec),
         scratch_shapes=[
             pltpu.VMEM((slots * slot, LANE), f32),
+            pltpu.VMEM((slots * 2 * plane, LANE), f32),
             pltpu.VMEM((MECH * block, LANE), f32),
             pltpu.VMEM((block, LANE), f32),
             pltpu.VMEM((block, LANE), f32),
@@ -288,11 +350,16 @@
             pltpu.VMEM((block, LANE), f32),
             pltpu.VMEM((slots, 2, cz, xt, LANE), f32),
             pltpu.VMEM((slots, 2, cz, xt, LANE), f32),
+            pltpu.VMEM((TIME, recs), f32),
+            pltpu.VMEM((n_dev * TIME, recs), f32),
+            pltpu.VMEM((n_dev * recs, recs), jnp.bfloat16),
             pltpu.SemaphoreType.DMA((6,)),
             pltpu.SemaphoreType.DMA((2, 2, yt)),
             pltpu.SemaphoreType.DMA((2, 2, yt)),
             pltpu.SemaphoreType.DMA((2, 2, 2)),
             pltpu.SemaphoreType.DMA((2, 2, 2)),
+            pltpu.SemaphoreType.DMA((n_dev,)),
+            pltpu.SemaphoreType.DMA((n_dev,)),
             pltpu.SemaphoreType.DMA,
         ],
         compiler_params=pltpu.CompilerParams(
@@ -310,20 +377,17 @@
     ):
         cz, cy, nx = pressure.shape
         corners, recs = receiver_cell.shape
-        decays = jnp.exp(-1.0 / relax_time)
         x = receiver_cell % nx
         y = (receiver_cell // nx) % cy
         z = receiver_cell // (nx * cy)
         rows = ((z * (cy // SUB) + y // SUB) * (nx // LANE) + x // LANE) * SUB + y % SUB
         run = make_kernel(cz, cy, nx, n_gz, n_gy, corners, recs)
-        samples, out = run(
+        traces, out = run(
             to_rows(pressure), to_rows(previous), to_rows(memory), to_rows(courant),
-            to_rows(quality), to_rows(sponge), decays,
+            to_rows(quality), to_rows(sponge), relax_time,
             rows.reshape(-1), (x % LANE).reshape(-1), receiver_weight.reshape(-1),
+            output_order[None, :],
         )
-        collected = lax.all_gather(samples, ("gz", "gy"), axis=1, tiled=True)
-        pick = lax.broadcasted_iota(jnp.int32, (collected.shape[1], recs), 0) == output_order[None, :]
-        traces = jnp.dot(collected, pick.astype(jnp.float32), precision=lax.Precision.HIGHEST)
         return traces, from_rows(out, (cz, cy, nx))
 
     in_specs = (

time: 123 us -> 109 us (0.89)
  blocking collectives: 20.5 us -> 0 us
  Pallas kernels: 95.8 us -> 104 us
  local copies, waits for them, and re-layouts: 2.29 us -> 3.59 us
    all_gather x1 -> x0, blocking collectives: 20.5 us -> none  [on_device(): collected = lax.all_gather(samples, ('gz', 'gy'), axis=1, tiled=True)]
    pallas_call x1, Pallas kernels: 95.8 us -> 104 us  [on_device(): run(to_rows(pressure), to_rows(previous), to_rows(memory), to_rows(couran...]
    unnamed x3 -> x2, local copies, waits for them, and re-layouts: 2.29 us -> 3.59 us
where the time goes in v2:
time: 109 us
  Pallas kernels  104 us (95%)
  local copies, waits for them, and re-layouts  3.59 us (3%)
  other arithmetic  1.31 us (1%)
    pallas_call x1, Pallas kernels, on_device(): run(to_rows(pressure), to_rows(previous), to_rows(memory), to_rows(couran...  104 us
    unnamed x2, local copies, waits for them, and re-layouts  3.59 us

profile of v2, /device:TPU:0, one launch (start us, length us, event | category | flops | bytes accessed | tf_op | source)
XLA Modules:
  0.0 109.2 jit_solution(1910106874885097573)
XLA Ops:
  0.6 1.3 %fusion.9 = (s32[1024]{0:T(1024)}, s32[1024]{0:T(1024)}) fusion(s32[8,128]{1,0:T(8,128)} %param.17), kind=kLoop, calls=%fused_computation.30 | loop fusion | flops 86016 | bytes 12288 | tf_op jit(solution)/shard_map/reshape | solution.py:388
  1.9 103.6 %shard_map.113 = (f32[24,128]{1,0:T(8,128)}, f32[2048,128]{1,0:T(8,128)}) custom-call(f32[2048,128]{1,0:T(8,128)} %bitcast.42, f32[2048,128]{1,0:T(8,128)} %bitcast.43, f32[6144,128]{1,0:T(8,128)} %bitcast.41, f32[2048,128]{1,0:T(8,128)} %bitcast.44, f32[2048,128]{1,0:T(8,128)} %bitcast.45, s32[2048,128]{1,0:T(8,128)} %bitcast.46, f32[3]{0:T(128)} %relax.1, ...), custom_call_target="tpu_custom_call" | custom-call | tf_op jit(solution)/shard_map/pallas_call | solution.py:385
  105.6 1.3 %copy.14 = f32[24,128]{1,0:T(8,128)} copy(f32[24,128]{1,0:T(8,128)} %get-tuple-element.10) | data formatting | bytes 24576
  106.9 2.3 %copy.15 = f32[16,32,512]{2,1,0:T(8,128)} copy(f32[16,32,512]{2,1,0:T(8,128)} %bitcast.47) | data formatting | bytes 2097152
